TPU v7x, 32 devices: a whole 2x2x4 slice. The times are simulated.
32 devices in a mesh: grp: 4 (over z), fsdp: 4 (over y, x), tp: 2 (over core).
Axes of the slice: x: 2, y: 2, z: 4, core: 2. Of those that a mesh axis runs over, the one named last changes fastest.
Arguments:
- frames: bfloat16 [768, 5120], P('fsdp', 'grp'), may hold values from -6 to 6
- projector: bfloat16 [5120, 8192], P('grp', 'tp'), may hold values from -0.078125 to 0.078125
- text_token_embedding: bfloat16 [4096, 8192], P(('grp', 'fsdp'), 'tp'), may hold values from -6 to 6
- norm_gain_vector: float32 [8192], replicated, may hold values from 0.1 to 1.9
- frozen: bfloat16 [8192, 1024], P('fsdp', 'tp'), may hold values from -0.0625 to 0.0625
- adapter_down_map: bfloat16 [8192, 64], P('fsdp'), may hold values from -0.0625 to 0.0625
- adapter_up_map: bfloat16 [64, 1024], P(None, 'tp'), may hold values from -0.75 to 0.75
- clip_frame_length: int32 [4, 4, 4], P('fsdp'), may hold values from 1 to 24, as said below
- audio_first_token: int32 [4, 4, 4], P('fsdp'), may hold values from 0 to 255, as said below
- segment_document_index: int32 [4096], P(('grp', 'fsdp')), may hold values from 0 to 63, never falling along the last dimension, each value on 1 to 256 neighbouring positions
- keep_document_flags: int32 [64], replicated, may hold values 0 or 1
- cotangent: bfloat16 [4096, 1024], P(('grp', 'fsdp'), 'tp'), may hold values from -0.09375 to 0.09375
Outputs:
- value_output: bfloat16 [4096, 1024], P(('grp', 'fsdp'), 'tp')
- projector_grad: float32 [5120, 8192], P('grp', 'tp')
- down_map_gradient: float32 [8192, 64], P('tp')
- up_map_gradient: float32 [64, 1024], P(None, 'tp')
Inputs may be any that keep to these rules, and one draw needn't show every extreme that they name: `clip_frame_length`: entry [f, g, k] is the length of clip k of frame block f * 4 + g; the 4 clips of a block sum to 48, and one of them has exactly 24 frames. `audio_first_token`: entry [f, g, k] is the first token, among the 256 tokens of block k * 4 + f, of the audio slots of clip k of frame block f * 4 + g; the 4 clips that one token block takes lie in distinct aligned windows of 64 tokens.
All inputs are finite; a program needn't handle non-finite values.
Results may differ from a plain program's by a relative error of at most 0.018.
Values may be sent and summed in bfloat16 or wider, within the bound.
A program may use at most 128 MiB of HBM per device.

v0:
```python
import jax
import jax.numpy as jnp
from jax import lax
from jax.sharding import PartitionSpec as P

adapter_scale = 2.0
norm_eps = 1e-05
plane = ("fsdp", "tp")


def contract_leading(left_side, right_side):
    return lax.dot_general(
        left_side, right_side, (((0,), (0,)), ((), ())), preferred_element_type=jnp.float32
    )


def contract_trailing(left_side, right_side):
    return lax.dot_general(
        left_side, right_side, (((1,), (1,)), ((), ())), preferred_element_type=jnp.float32
    )


def block_perm(f_size, t_size, shift):
    pairs = []
    for f_src in range(f_size):
        for t_src in range(t_size):
            b = f_src * t_size + (t_src + shift) % t_size
            pairs.append((f_src * t_size + t_src, b % f_size * t_size + b // f_size))
    return pairs


def shards(
    frames,
    projector,
    text_token_embedding,
    norm_gain_vector,
    frozen,
    adapter_down_map,
    adapter_up_map,
    clip_frame_length,
    audio_first_token,
    segment_document_index,
    keep_document_flags,
    cotangent,
):
    g_idx, f_idx, t_idx = (lax.axis_index("grp"), lax.axis_index("fsdp"), lax.axis_index("tp"))
    f_size, t_size = (lax.axis_size("fsdp"), lax.axis_size("tp"))
    tok, width = text_token_embedding.shape
    groups = clip_frame_length.shape[1]
    block_frames = frames.shape[0]
    per_group = block_frames // groups
    cols = width // f_size
    full_width = width * t_size
    v_shard = frozen.shape[1]
    v_full = v_shard * t_size
    rank = adapter_down_map.shape[1]
    frames_all = lax.all_gather(frames, "fsdp", axis=0, tiled=True)
    clips = lax.all_gather(jnp.stack([clip_frame_length[0], audio_first_token[0]]), "fsdp", axis=0)
    text = lax.all_to_all(
        text_token_embedding.reshape(tok, f_size, cols).transpose(1, 0, 2),
        "fsdp",
        split_axis=0,
        concat_axis=0,
        tiled=True,
    )
    own_block = t_idx * f_size + f_idx
    own_j = lax.rem(own_block, t_size)
    frozen_own = jnp.zeros((cols, v_full), jnp.bfloat16)
    for shift in range(t_size):
        j = lax.rem(t_idx + shift, t_size)
        piece = lax.ppermute(
            lax.dynamic_slice_in_dim(frozen, j * cols, cols, 0),
            plane,
            block_perm(f_size, t_size, shift),
        )
        t_src = lax.rem(own_j - shift + t_size, t_size)
        frozen_own = lax.dynamic_update_slice_in_dim(frozen_own, piece, t_src * v_shard, 1)
    down_own = lax.ppermute(
        lax.dynamic_slice_in_dim(adapter_down_map, t_idx * cols, cols, 0),
        plane,
        block_perm(f_size, t_size, 0),
    )
    gain_own = lax.dynamic_slice_in_dim(norm_gain_vector, t_idx * width + f_idx * cols, cols, 0)
    sizes, firsts = (clips[:, 0], clips[:, 1])
    ends = jnp.cumsum(sizes, axis=2)
    pick = lax.broadcasted_iota(jnp.int32, sizes.shape, 2) == g_idx
    size_in = jnp.sum(jnp.where(pick, sizes, 0), axis=2)
    start_in = jnp.sum(jnp.where(pick, ends - sizes, 0), axis=2)
    first_in = jnp.sum(jnp.where(pick, firsts, 0), axis=2)
    base_row = lax.broadcasted_iota(jnp.int32, size_in.shape, 1) * per_group + start_in
    token_iota = lax.broadcasted_iota(jnp.int32, (f_size, tok, groups), 1)
    offset = token_iota - first_in[:, None, :]
    live = (offset >= 0) & (offset < size_in[:, None, :])
    is_audio = jnp.any(live, axis=2)
    row = jnp.sum(jnp.where(live, base_row[:, None, :] + offset, 0), axis=2)
    row = jnp.where(is_audio, row, -1)
    frame_iota = lax.broadcasted_iota(jnp.int32, (f_size, tok, block_frames), 2)
    take = (row[:, :, None] == frame_iota).astype(jnp.bfloat16)
    take_own = lax.dynamic_index_in_dim(take, f_idx, 0, keepdims=False)
    doc_iota = lax.broadcasted_iota(jnp.int32, (tok, keep_document_flags.shape[0]), 1)
    weight_tok = jnp.sum(
        jnp.where(segment_document_index[:, None] == doc_iota, keep_document_flags[None, :], 0),
        axis=1,
    )
    grad_out = cotangent * weight_tok.astype(jnp.bfloat16)[:, None]
    both = lax.all_gather(
        jnp.concatenate([grad_out, adapter_up_map], axis=0), "tp", axis=1, tiled=True
    )
    grad_full, up_full = (both[:tok], both[tok:])
    lora_tok = (adapter_scale * contract_trailing(grad_full, up_full)).astype(jnp.bfloat16)
    lora_plane = lax.all_gather(lora_tok, "fsdp", axis=0, tiled=True)
    grad_rows = lax.psum(contract_leading(take_own, grad_full).astype(jnp.bfloat16), "grp")
    grad_rows = lax.all_gather(grad_rows, "fsdp", axis=0, tiled=True)
    lora_rows = (adapter_scale * contract_trailing(grad_rows, up_full)).astype(jnp.bfloat16)
    grad_norm = contract_trailing(grad_rows, frozen_own) + contract_trailing(lora_rows, down_own)
    projector_own = lax.dynamic_slice_in_dim(projector, f_idx * cols, cols, 1)
    embedded = lax.psum(
        jnp.dot(frames_all, projector_own, preferred_element_type=jnp.float32).astype(jnp.bfloat16),
        "grp",
    )
    audio = lax.dot_general(
        take,
        embedded.reshape(f_size, block_frames, cols),
        (((2,), (1,)), ((0,), (0,))),
        preferred_element_type=jnp.float32,
    ).astype(jnp.bfloat16)
    x = jnp.where(is_audio[:, :, None], audio, text).reshape(f_size * tok, cols)
    x32 = x.astype(jnp.float32)
    e32 = embedded.astype(jnp.float32)
    stats = lax.psum(
        jnp.concatenate(
            [
                jnp.sum(x32 * x32, axis=1),
                jnp.sum(e32 * e32, axis=1),
                jnp.sum(e32 * gain_own[None, :] * grad_norm, axis=1),
            ]
        ),
        plane,
    )
    n_tok, n_frames = (f_size * tok, f_size * block_frames)
    inv_tok = lax.rsqrt(stats[:n_tok] / full_width + norm_eps)
    inv_frame = lax.rsqrt(stats[n_tok : n_tok + n_frames] / full_width + norm_eps)
    dots = inv_frame * stats[n_tok + n_frames :]
    frame_grad = (
        inv_frame[:, None] * gain_own[None, :] * grad_norm
        - e32 * (inv_frame * inv_frame * dots / full_width)[:, None]
    ).astype(jnp.bfloat16)
    frame_grad = lax.all_gather(frame_grad, "fsdp", axis=1, tiled=True)
    projector_grad = contract_leading(frames_all, frame_grad)
    normed = (x32 * inv_tok[:, None] * gain_own[None, :]).astype(jnp.bfloat16)
    low_part = jnp.dot(normed, down_own, preferred_element_type=jnp.float32)
    value_part = jnp.dot(normed, frozen_own, preferred_element_type=jnp.float32)
    value_part = value_part + adapter_scale * jnp.dot(
        low_part.astype(jnp.bfloat16), up_full, preferred_element_type=jnp.float32
    )
    value_part = value_part.astype(jnp.bfloat16).reshape(f_size, tok, t_size, v_shard)
    low_send = jnp.broadcast_to(
        low_part.astype(jnp.bfloat16).reshape(f_size, tok, 1, rank), (f_size, tok, t_size, rank)
    )
    sent = (
        jnp.concatenate([value_part, low_send], axis=3)
        .transpose(0, 2, 1, 3)
        .reshape(f_size * t_size, tok, v_shard + rank)
    )
    got = lax.all_to_all(sent, plane, split_axis=0, concat_axis=0, tiled=True)
    total = jnp.sum(got.astype(jnp.float32), axis=0)
    value_output = total[:, :v_shard].astype(jnp.bfloat16)
    low_half = total[:, v_shard:].astype(jnp.bfloat16)
    up_part = adapter_scale * contract_leading(low_half, grad_out)
    down_part = contract_leading(normed, lora_plane)
    down_sum, up_sum = lax.psum((down_part, up_part), "grp")
    gathered = lax.all_gather(
        jnp.concatenate([down_sum, up_sum.reshape(-1, rank)], axis=0), "fsdp", axis=0
    )
    down_map_gradient = gathered[:, :cols].reshape(width, rank)
    up_map_gradient = jnp.sum(gathered[:, cols:], axis=0).reshape(rank, v_shard)
    return (value_output, projector_grad, down_map_gradient, up_map_gradient)


def solution(mesh):
    in_specs = (
        P("fsdp", "grp"),
        P("grp", "tp"),
        P(("grp", "fsdp"), "tp"),
        P(),
        P("fsdp", "tp"),
        P("fsdp", None),
        P(None, "tp"),
        P("fsdp", None, None),
        P("fsdp", None, None),
        P(("grp", "fsdp")),
        P(),
        P(("grp", "fsdp"), "tp"),
    )
    out_specs = (P(("grp", "fsdp"), "tp"), P("grp", "tp"), P("tp", None), P(None, "tp"))
    return jax.shard_map(shards, mesh=mesh, in_specs=in_specs, out_specs=out_specs, check_vma=False)
```

profile of v0, /device:TPU:0, one launch (start us, length us, event | category | flops | bytes accessed | tf_op | source)
XLA Modules:
  0.0 499.5 jit_solution(9193602135876863072)
XLA Ops:
  7.2 0.7 all-gather.7.cloned.1.call-update
  8.0 0.8 select_reduce_fusion
  8.8 0.7 pad_add_fusion
  9.5 9.7 %all-gather = s32[8,4,4]{2,1,0:T(4,128)S(1)} all-gather(s32[2,4,4]{2,1,0:T(4,128)S(1)} %pad_add_fusion), channel_id=2, replica_groups=mesh['grp'=4,'fsdp'=4,'tp'=2] {'fsdp'}, dimensions={0}, use_global_device_ids=true | all-gather | bytes 640 | tf_op jit(solution)/shard_map/all_gather | solution.py:58
  19.2 0.7 reduce_window_sum.11
  19.9 0.3 select_reduce_fusion.2
  20.2 0.1 fusion.42
  20.3 0.1 select_reduce_fusion.1
  20.4 1.1 broadcast_multiply_fusion
  21.5 0.9 pad_maximum_fusion.2
  22.4 2.3 all_gather.30
  24.6 0.1 iota_compare_fusion
  24.7 1.0 convolution_convert_fusion
  25.8 20.9 %all-gather.7.cloned.1.call-done = bf16[768,1280]{1,0:T(8,128)(2,1)} async-done(((bf16[192,1280]{1,0:T(8,128)(2,1)}), bf16[768,1280]{1,0:T(8,128)(2,1)}) %all-gather.7.cloned.1.call-update) | async-done | bytes 1966096 | tf_op jit(solution)/shard_map/all_gather | solution.py:57
  46.7 5.7 %fusion.12 = bf16[768,1024]{0,1:T(8,128)(2,1)} fusion(bf16[768,1280]{1,0:T(8,128)(2,1)} %all-gather.7.cloned.1.call-done, bf16[1280,4096]{1,0:T(8,128)(2,1)} %param.13, s32[]{:T(128)S(6)} %select_n.60), kind=kOutput, calls=%fused_computation.20 | convolution fusion | flops 2014052352 | bytes 6160388 | tf_op jit(solution)/shard_map/dot_general | solution.py:118
  52.5 82.0 %all-reduce.7.cloned.1.call-done = (bf16[768,1024]{0,1:T(8,128)(2,1)}, bf16[192,1024]{1,0:T(8,128)(2,1)}) async-done(((bf16[768,1024]{0,1:T(8,128)(2,1)}, bf16[192,1024]{1,0:T(8,128)(2,1)}), (bf16[768,1024]{0,1:T(8,128)(2,1)}, bf16[192,1024]{1,0:T(8,128)(2,1)})) %all-reduce.7.cloned.1.call-update) | async-done | bytes 1966096 | tf_op jit(solution)/shard_map/psum | solution.py:117
  134.5 3.3 copy.56
  137.8 2.4 copy.57
  140.2 3.6 all-to-all-start
  143.8 3.0 constant_dynamic-slice_fusion
  146.8 9.4 %collective-permute-start = (bf16[1024,512]{1,0:T(8,128)(2,1)}, bf16[1024,512]{1,0:T(8,128)(2,1)}, u32[]{:S(2)}, u32[]{:S(2)}) collective-permute-start(bf16[1024,512]{1,0:T(8,128)(2,1)} %get-tuple-element.30), channel_id=1, source_target_pairs={{0,0},{1,2},{2,4},{3,6},{4,1},{5,3},{6,5},{7,7},{8,8},{9,10},{10,1... | collective-permute-start | bytes 3145736 | tf_op jit(solution)/shard_map/ppermute | solution.py:71
  156.3 0.7 collective-permute-start.2
  157.0 0.7 dynamic_slice.20
  157.7 1.6 broadcast_in_dim.61
  159.3 2.3 constant_dynamic-update-slice_fusion.1
  161.6 40.1 %collective-permute-done.1 = bf16[1024,512]{1,0:T(8,128)(2,1)} collective-permute-done((bf16[1024,512]{1,0:T(8,128)(2,1)}, bf16[1024,512]{1,0:T(8,128)(2,1)}, u32[]{:S(2)}, u32[]{:S(2)}) %collective-permute-start.1) | collective-permute-done | bytes 1048608 | tf_op jit(solution)/shard_map/ppermute | solution.py:71
  201.7 2.3 constant_dynamic-update-slice_fusion
  204.0 2.6 copy.55
  206.6 4.5 multiply_reduce_fusion
  211.2 4.3 fusion.16
  215.5 6.7 %fusion.2 = (f32[768]{0:T(1024)S(1)}, f32[768]{0:T(1024)S(1)}, f32[768,1024]{0,1:T(8,128)}) fusion(bf16[768,1024]{0,1:T(8,128)(2,1)S(1)} %copy-done.2, f32[1024]{0:T(1024)S(1)} %dynamic_slice.20, f32[768,1024]{0,1:T(8,128)} %fusion.16, bf16[768,1024]{1,0:T(8,128)(2,1)} %all-gather.9.cloned.1.call-done, bf16[1024,1024]{1,0:T(8,128)(2,1)} %constant_dynamic-update-slice_fusion), kind=kOutput, calls=%fused_computation.9 | convolution fusion | flops 1616116224 | bytes 11544576 | tf_op jit(solution)/shard_map/dot_general | solution.py:18
  222.2 27.2 %psum.37 = f32[2560]{0:T(1024)S(1)} all-reduce(f32[2560]{0:T(1024)S(1)} %pad_maximum_fusion.3), channel_id=1, replica_groups=mesh['grp'=4,'fsdp'=4,'tp'=2] {'fsdp','tp'}, use_global_device_ids=true, to_apply=%region_12.13 | all-reduce | flops 2560 | bytes 20480 | tf_op jit(solution)/shard_map/psum | solution.py:130
  249.3 2.6 fusion.1
  252.0 0.8 convolution_convert_fusion.1
  252.7 0.7 fusion.23
  253.5 5.3 %add_convert_fusion = bf16[1024,1024]{1,0:T(8,128)(2,1)} fusion(f32[1024,1024]{1,0:T(8,128)S(1)} %fusion.23, bf16[1024,1024]{1,0:T(8,128)(2,1)S(1)} %fusion.1, bf16[1024,1024]{1,0:T(8,128)(2,1)} %constant_dynamic-update-slice_fusion), kind=kOutput, calls=%fused_computation.7 | convolution fusion | flops 2150629376 | bytes 10485760 | tf_op jit(solution)/shard_map/dot_general | solution.py:152
  258.7 4.5 reshape.66
  263.2 6.1 %copy.61 = bf16[4,256,2,512]{1,3,2,0:T(8,128)(2,1)} copy(bf16[4,256,2,512]{3,2,1,0:T(2,128)(2,1)} %reshape.66) | data formatting | bytes 4194304 | tf_op jit(solution)/shard_map/reshape | solution.py:156
  269.4 3.2 pad_maximum_fusion
  272.5 4.4 all-to-all-start.1
  276.9 0.0 all-reduce.5.cloned.1.call-start
  277.0 0.3 fusion.17
  277.2 32.5 %all_gather.33 = bf16[1024,64]{0,1:T(8,128)(2,1)S(1)} all-gather(bf16[256,64]{0,1:T(8,128)(2,1)S(1)} %fusion.17), channel_id=1, replica_groups=mesh['grp'=4,'fsdp'=4,'tp'=2] {'fsdp'}, dimensions={0}, use_global_device_ids=true | all-gather | bytes 163840 | tf_op jit(solution)/shard_map/all_gather | solution.py:111
  309.8 1.2 fusion.44
  311.0 2.2 reduce.1
  313.2 0.2 convolution_multiply_fusion.1
  313.4 0.1 reshape.68
  313.5 0.8 copy.62
  314.3 0.0 all-gather.13.cloned.1.call-start
  314.3 35.8 %all-reduce.5.cloned.1.call-done = (f32[512,64]{0,1:T(8,128)}, f32[1024,64]{0,1:T(8,128)}) async-done(((f32[512,64]{0,1:T(8,128)}, f32[1024,64]{0,1:T(8,128)}), (f32[512,64]{0,1:T(8,128)}, f32[1024,64]{0,1:T(8,128)})) %all-reduce.5.cloned.1.call-update) | async-done | bytes 393232 | tf_op jit(solution)/shard_map/psum | solution.py:171
  350.1 1.8 pad_maximum_fusion.1
  351.9 0.3 all-gather.11.cloned.1.call-start
  352.2 3.6 fusion.6
  355.9 0.8 copy.64
  356.7 26.3 %all-gather.13.cloned.1.call-done = f32[6144,64]{0,1:T(8,128)} async-done(((f32[1536,64]{0,1:T(8,128)}), f32[6144,64]{0,1:T(8,128)}) %all-gather.13.cloned.1.call-update) | async-done | bytes 1572880 | tf_op jit(solution)/shard_map/all_gather | solution.py:172
  383.0 2.4 reshape.73
  385.4 0.1 slice.55
  385.6 1.6 copy.70
  387.1 0.2 slice_reduce_fusion
  387.4 0.1 copy.63
  387.5 0.8 reshape.70
  388.3 67.0 %all-gather.11.cloned.1.call-done = bf16[768,4096]{0,1:T(8,128)(2,1)} async-done(((bf16[768,1024]{0,1:T(8,128)(2,1)}), bf16[768,4096]{0,1:T(8,128)(2,1)}) %all-gather.11.cloned.1.call-update) | async-done | bytes 6291472 | tf_op jit(solution)/shard_map/all_gather | solution.py:148
  455.3 14.9 %convolution_bitcast_fusion = f32[1280,4096]{0,1:T(8,128)} fusion(bf16[768,4096]{0,1:T(8,128)(2,1)} %all-gather.11.cloned.1.call-done, bf16[768,1280]{1,0:T(8,128)(2,1)} %all-gather.7.cloned.1.call-done), kind=kOutput, calls=%fused_computation | convolution fusion | flops 8053063680 | bytes 29229056 | tf_op jit(solution)/shard_map/dot_general | solution.py:12
  470.2 22.4 %copy.65 = f32[1280,4096]{1,0:T(8,128)} copy(f32[1280,4096]{0,1:T(8,128)} %convolution_bitcast_fusion) | data formatting | bytes 41943040
  (38 shorter events, 0.4 us)
Async XLA Ops:
  7.2 149.1 %copy-start = (bf16[2048,64]{0,1:T(8,128)(2,1)S(1)}, bf16[2048,64]{0,1:T(8,128)(2,1)}, u32[]{:S(2)}) copy-start(bf16[2048,64]{0,1:T(8,128)(2,1)} %param.17) | copy-start | bytes 786436
  7.2 39.5 %all-gather.7.cloned.1.call-start = ((), (), s32[]{:S(2)}) async-start(), calls=%async_computation.2 | async-start | bytes 2457600 | tf_op jit(solution)/shard_map/all_gather | solution.py:57
  7.9 126.6 %all-reduce.7.cloned.1.call-start = ((), (), s32[]{:S(2)}) async-start(), calls=%async_computation.7 | async-start | bytes 3932160 | tf_op jit(solution)/shard_map/psum | solution.py:117
  52.5 158.7 %all-gather.9.cloned.1.call-start = ((), (), s32[]{:S(2)}) async-start(), calls=%async_computation.3 | async-start | bytes 1966080 | tf_op jit(solution)/shard_map/all_gather | solution.py:113
  140.2 66.4 %all-to-all-start = ((bf16[4,256,1024]{2,1,0:T(8,128)(2,1)}), bf16[4,256,1024]{2,1,0:T(8,128)(2,1)S(1)}, u32[]{:S(2)}, u32[]{:S(2)}) async-start(bf16[4,256,1024]{2,1,0:T(8,128)(2,1)} %bitcast.60), calls=%async_computation | async-start | bytes 4194304 | tf_op jit(solution)/shard_map/all_to_all | solution.py:59
  146.8 10.9 %collective-permute-start = (bf16[1024,512]{1,0:T(8,128)(2,1)}, bf16[1024,512]{1,0:T(8,128)(2,1)}, u32[]{:S(2)}, u32[]{:S(2)}) collective-permute-start(bf16[1024,512]{1,0:T(8,128)(2,1)} %get-tuple-element.30), channel_id=1, source_target_pairs={{0,0},{1,2},{2,4},{3,6},{4,1},{5,3},{6,5},{7,7},{8,8},{9,10},{10,1... | collective-permute-start | bytes 3145736 | tf_op jit(solution)/shard_map/ppermute | solution.py:71
  156.3 45.4 %collective-permute-start.1 = (bf16[1024,512]{1,0:T(8,128)(2,1)}, bf16[1024,512]{1,0:T(8,128)(2,1)}, u32[]{:S(2)}, u32[]{:S(2)}) collective-permute-start(bf16[1024,512]{1,0:T(8,128)(2,1)} %get-tuple-element.29), channel_id=1, source_target_pairs={{0,2},{1,0},{2,6},{3,4},{4,3},{5,1},{6,7},{7,5},{8,10},{9,8},{10,1... | collective-permute-start | bytes 3145736 | tf_op jit(solution)/shard_map/ppermute | solution.py:71
  156.3 54.8 %collective-permute-start.2 = (bf16[1024,64]{0,1:T(8,128)(2,1)S(1)}, bf16[1024,64]{0,1:T(8,128)(2,1)S(1)}, u32[]{:S(2)}, u32[]{:S(2)}) collective-permute-start(bf16[1024,64]{0,1:T(8,128)(2,1)S(1)} %constant_dynamic-slice_fusion.2), channel_id=1, source_target_pairs={{0,0},{1,2},{2,4},{3,6},{4,1},{5,3},{6,5},{7,7},{8,8},{9,10},{10,1... | collective-permute-start | bytes 393224 | tf_op jit(solution)/shard_map/ppermute | solution.py:78
  211.1 4.3 copy-start.2
  272.5 38.4 %all-to-all-start.1 = ((bf16[8,256,576]{1,2,0:T(8,128)(2,1)}), bf16[8,256,576]{1,2,0:T(8,128)(2,1)}, u32[]{:S(2)}, u32[]{:S(2)}) async-start(bf16[8,256,576]{1,2,0:T(8,128)(2,1)} %bitcast.59), calls=%async_computation.1 | async-start | bytes 4718592 | tf_op jit(solution)/shard_map/all_to_all | solution.py:165
  276.9 73.2 %all-reduce.5.cloned.1.call-start = ((), (), s32[]{:S(2)}) async-start(), calls=%async_computation.6 | async-start | bytes 786432 | tf_op jit(solution)/shard_map/psum | solution.py:171
  310.9 41.2 %copy-start.3 = (bf16[768,1024]{0,1:T(8,128)(2,1)S(1)}, bf16[768,1024]{0,1:T(8,128)(2,1)}, u32[]{:S(2)}) copy-start(bf16[768,1024]{0,1:T(8,128)(2,1)} %get-tuple-element.27) | copy-start | bytes 4718596
  314.3 68.8 %all-gather.13.cloned.1.call-start = ((), (), s32[]{:S(2)}) async-start(), calls=%async_computation.5 | async-start | bytes 1966080 | tf_op jit(solution)/shard_map/all_gather | solution.py:172
  351.9 103.4 %all-gather.11.cloned.1.call-start = ((), (), s32[]{:S(2)}) async-start(), calls=%async_computation.4 | async-start | bytes 7864320 | tf_op jit(solution)/shard_map/all_gather | solution.py:148
  470.2 22.4 %copy-start.1 = (bf16[2048,64]{0,1:T(8,128)(2,1)S(1)}, bf16[2048,64]{0,1:T(8,128)(2,1)}, u32[]{:S(2)}) copy-start(bf16[2048,64]{0,1:T(8,128)(2,1)} %param.17) | copy-start | bytes 786436
Sparse Core Ops, SparseCore 0:
  9.8 36.8 all-gather.6
  52.6 81.8 all-reduce.6
  136.3 52.9 all-gather.8
  314.4 35.6 all-reduce.4
  352.3 30.6 all-gather.12
  385.3 70.0 all-gather.10
where the time goes:
time: 502 us; the launch traced here: 499 us
  waiting for transfers between devices  273 us (54%)
  blocking collectives  71.6 us (14%)
  local copies, waits for them, and re-layouts  58.1 us (12%)
  matrix products  45.5 us (9%)
  starting transfers between devices  18.6 us (4%)
  other arithmetic  18.5 us (4%)
  between operations  14.3 us (3%)
    psum x1, waiting for transfers between devices, shards(): lax.psum(jnp.dot(frames_all, projector_own, preferred_element_type=jnp.fl...  82 us
    all_gather x1, waiting for transfers between devices, shards(): frame_grad = lax.all_gather(frame_grad, 'fsdp', axis=1, tiled=True)  67 us
    ppermute x2, waiting for transfers between devices, shards(): lax.ppermute(lax.dynamic_slice_in_dim(frozen, j * cols, cols, 0), plane,...  40.1 us
    psum x1, waiting for transfers between devices, shards(): down_sum, up_sum = lax.psum((down_part, up_part), 'grp')  35.8 us
    all_gather x1, blocking collectives, shards(): lora_plane = lax.all_gather(lora_tok, 'fsdp', axis=0, tiled=True)  32.5 us
    unnamed x13, local copies, waits for them, and re-layouts  28.2 us
    psum x1, blocking collectives, shards(): lax.psum(jnp.concatenate([jnp.sum(x32 * x32, axis=1), jnp.sum(e32 * e32,...  27.2 us
    all_gather x1, waiting for transfers between devices, shards(): lax.all_gather(jnp.concatenate([down_sum, up_sum.reshape(-1, rank)], axis...  26.3 us
  transfers between devices with their start and end apart: 11, of which 6 were waited for; matrix products, arithmetic and copies ran while one was open for 8% of the time, Pallas kernels for 0%

commit v1 on v0

--- a/solution.py
+++ b/solution.py
@@ -145,7 +145,15 @@
         inv_frame[:, None] * gain_own[None, :] * grad_norm
         - e32 * (inv_frame * inv_frame * dots / full_width)[:, None]
     ).astype(jnp.bfloat16)
-    frame_grad = lax.all_gather(frame_grad, "fsdp", axis=1, tiled=True)
+    frame_grad = jnp.concatenate(
+        lax.all_to_all(
+            jnp.stack(lax.axis_size("fsdp") * [frame_grad]),
+            axis_name="fsdp",
+            split_axis=0,
+            concat_axis=0,
+        ),
+        axis=1,
+    )
     projector_grad = contract_leading(frames_all, frame_grad)
     normed = (x32 * inv_tok[:, None] * gain_own[None, :]).astype(jnp.bfloat16)
     low_part = jnp.dot(normed, down_own, preferred_element_type=jnp.float32)

time: 502 us -> 484 us (0.964)
  waiting for transfers between devices: 273 us -> 206 us
  blocking collectives: 71.6 us -> 111 us
    all_gather x1 -> x0, waiting for transfers between devices: 67 us -> none  [shards(): frame_grad = lax.all_gather(frame_grad, 'fsdp', axis=1, tiled=True)]
    all_gather x1, blocking collectives: 32.5 us -> 72 us  [shards(): lora_plane = lax.all_gather(lora_tok, 'fsdp', axis=0, tiled=True)]
    all_gather x1, waiting for transfers between devices: 26.3 us -> 0.01 us  [shards(): lax.all_gather(jnp.concatenate([down_sum, up_sum.reshape(-1, rank)], axis...]
    all_to_all x1, waiting for transfers between devices: 0.01 us -> 25.3 us  [shards(): got = lax.all_to_all(sent, plane, split_axis=0, concat_axis=0, tiled=True)]
    all_to_all x0 -> x1, starting transfers between devices: none -> 5.26 us  [shards(): lax.all_to_all(jnp.stack(lax.axis_size('fsdp') * [frame_grad]), axis_name...]
  transfers between devices with their start and end apart: 11 -> 11, of which waited for: 6 -> 5; matrix products, arithmetic and copies ran while one was open for 8% -> 16% of each run, Pallas kernels for 0% -> 0%
where the time goes in v1:
time: 484 us; the launch traced here: 482 us
  waiting for transfers between devices  206 us (43%)
  blocking collectives  111 us (23%)
  local copies, waits for them, and re-layouts  62.6 us (13%)
  matrix products  45.3 us (9%)
  starting transfers between devices  23.6 us (5%)
  other arithmetic  18.8 us (4%)
  between operations  14 us (3%)
    psum x1, waiting for transfers between devices, shards(): lax.psum(jnp.dot(frames_all, projector_own, preferred_element_type=jnp.fl...  82 us
    all_gather x1, blocking collectives, shards(): lora_plane = lax.all_gather(lora_tok, 'fsdp', axis=0, tiled=True)  72 us
    ppermute x2, waiting for transfers between devices, shards(): lax.ppermute(lax.dynamic_slice_in_dim(frozen, j * cols, cols, 0), plane,...  40.1 us
    psum x1, waiting for transfers between devices, shards(): down_sum, up_sum = lax.psum((down_part, up_part), 'grp')  37.2 us
    unnamed x13, local copies, waits for them, and re-layouts  28.1 us
    psum x1, blocking collectives, shards(): lax.psum(jnp.concatenate([jnp.sum(x32 * x32, axis=1), jnp.sum(e32 * e32,...  27.2 us
    all_to_all x1, waiting for transfers between devices, shards(): got = lax.all_to_all(sent, plane, split_axis=0, concat_axis=0, tiled=True)  25.3 us
    all_gather x1, waiting for transfers between devices, shards(): frames_all = lax.all_gather(frames, 'fsdp', axis=0, tiled=True)  20.9 us
  transfers between devices with their start and end apart: 11, of which 5 were waited for; matrix products, arithmetic and copies ran while one was open for 16% of the time, Pallas kernels for 0%

profile of v1, /device:TPU:0, one launch (start us, length us, event | category | flops | bytes accessed | tf_op | source)
XLA Modules:
  0.0 481.6 jit_solution(986597594225435443)
XLA Ops:
  7.2 0.7 all-gather.6.cloned.1.call-update
  8.0 0.8 select_reduce_fusion
  8.8 0.7 pad_add_fusion
  9.5 9.7 %all-gather = s32[8,4,4]{2,1,0:T(4,128)S(1)} all-gather(s32[2,4,4]{2,1,0:T(4,128)S(1)} %pad_add_fusion), channel_id=2, replica_groups=mesh['grp'=4,'fsdp'=4,'tp'=2] {'fsdp'}, dimensions={0}, use_global_device_ids=true | all-gather | bytes 640 | tf_op jit(solution)/shard_map/all_gather | solution.py:58
  19.2 0.7 reduce_window_sum.11
  19.9 0.3 select_reduce_fusion.2
  20.2 0.1 fusion.42
  20.3 0.1 select_reduce_fusion.1
  20.4 1.1 broadcast_multiply_fusion
  21.5 0.9 pad_maximum_fusion.2
  22.4 2.3 all_gather.27
  24.6 0.1 iota_compare_fusion
  24.7 1.0 convolution_convert_fusion
  25.8 20.9 %all-gather.6.cloned.1.call-done = bf16[768,1280]{1,0:T(8,128)(2,1)} async-done(((bf16[192,1280]{1,0:T(8,128)(2,1)}), bf16[768,1280]{1,0:T(8,128)(2,1)}) %all-gather.6.cloned.1.call-update) | async-done | bytes 1966096 | tf_op jit(solution)/shard_map/all_gather | solution.py:57
  46.7 5.7 %fusion.12 = bf16[768,1024]{0,1:T(8,128)(2,1)} fusion(bf16[768,1280]{1,0:T(8,128)(2,1)} %all-gather.6.cloned.1.call-done, bf16[1280,4096]{1,0:T(8,128)(2,1)} %param.13, s32[]{:T(128)S(6)} %select_n.60), kind=kOutput, calls=%fused_computation.20 | convolution fusion | flops 2014052352 | bytes 6160388 | tf_op jit(solution)/shard_map/dot_general | solution.py:118
  52.5 82.0 %all-reduce.7.cloned.1.call-done = (bf16[768,1024]{0,1:T(8,128)(2,1)}, bf16[192,1024]{1,0:T(8,128)(2,1)}) async-done(((bf16[768,1024]{0,1:T(8,128)(2,1)}, bf16[192,1024]{1,0:T(8,128)(2,1)}), (bf16[768,1024]{0,1:T(8,128)(2,1)}, bf16[192,1024]{1,0:T(8,128)(2,1)})) %all-reduce.7.cloned.1.call-update) | async-done | bytes 1966096 | tf_op jit(solution)/shard_map/psum | solution.py:117
  134.5 3.3 copy.57
  137.8 2.4 copy.58
  140.2 3.6 all-to-all-start
  143.8 3.0 constant_dynamic-slice_fusion
  146.8 9.4 %collective-permute-start = (bf16[1024,512]{1,0:T(8,128)(2,1)}, bf16[1024,512]{1,0:T(8,128)(2,1)}, u32[]{:S(2)}, u32[]{:S(2)}) collective-permute-start(bf16[1024,512]{1,0:T(8,128)(2,1)} %get-tuple-element.30), channel_id=1, source_target_pairs={{0,0},{1,2},{2,4},{3,6},{4,1},{5,3},{6,5},{7,7},{8,8},{9,10},{10,1... | collective-permute-start | bytes 3145736 | tf_op jit(solution)/shard_map/ppermute | solution.py:71
  156.3 0.7 collective-permute-start.2
  157.0 0.7 dynamic_slice.20
  157.7 1.6 broadcast_in_dim.61
  159.3 2.3 constant_dynamic-update-slice_fusion.1
  161.6 40.1 %collective-permute-done.1 = bf16[1024,512]{1,0:T(8,128)(2,1)} collective-permute-done((bf16[1024,512]{1,0:T(8,128)(2,1)}, bf16[1024,512]{1,0:T(8,128)(2,1)}, u32[]{:S(2)}, u32[]{:S(2)}) %collective-permute-start.1) | collective-permute-done | bytes 1048608 | tf_op jit(solution)/shard_map/ppermute | solution.py:71
  201.7 2.3 constant_dynamic-update-slice_fusion
  204.0 2.6 copy.56
  206.6 4.5 multiply_reduce_fusion
  211.2 4.3 fusion.16
  215.5 6.7 %fusion.2 = (f32[768]{0:T(1024)S(1)}, f32[768]{0:T(1024)S(1)}, f32[768,1024]{0,1:T(8,128)}) fusion(bf16[768,1024]{0,1:T(8,128)(2,1)S(1)} %copy-done.2, f32[1024]{0:T(1024)S(1)} %dynamic_slice.20, f32[768,1024]{0,1:T(8,128)} %fusion.16, bf16[768,1024]{1,0:T(8,128)(2,1)} %all-gather.8.cloned.1.call-done, bf16[1024,1024]{1,0:T(8,128)(2,1)} %constant_dynamic-update-slice_fusion), kind=kOutput, calls=%fused_computation.9 | convolution fusion | flops 1616116224 | bytes 11544576 | tf_op jit(solution)/shard_map/dot_general | solution.py:18
  222.2 27.2 %psum.37 = f32[2560]{0:T(1024)S(1)} all-reduce(f32[2560]{0:T(1024)S(1)} %pad_maximum_fusion.3), channel_id=1, replica_groups=mesh['grp'=4,'fsdp'=4,'tp'=2] {'fsdp','tp'}, use_global_device_ids=true, to_apply=%region_12.13 | all-reduce | flops 2560 | bytes 20480 | tf_op jit(solution)/shard_map/psum | solution.py:130
  249.3 2.6 fusion.1
  252.0 0.8 convolution_convert_fusion.1
  252.7 0.7 fusion.23
  253.5 5.3 %add_convert_fusion = bf16[1024,1024]{1,0:T(8,128)(2,1)} fusion(f32[1024,1024]{1,0:T(8,128)S(1)} %fusion.23, bf16[1024,1024]{1,0:T(8,128)(2,1)S(1)} %fusion.1, bf16[1024,1024]{1,0:T(8,128)(2,1)} %constant_dynamic-update-slice_fusion), kind=kOutput, calls=%fused_computation.7 | convolution fusion | flops 2150629376 | bytes 10485760 | tf_op jit(solution)/shard_map/dot_general | solution.py:160
  258.7 4.5 reshape.74
  263.2 6.1 %copy.62 = bf16[4,256,2,512]{1,3,2,0:T(8,128)(2,1)} copy(bf16[4,256,2,512]{3,2,1,0:T(2,128)(2,1)} %reshape.74) | data formatting | bytes 4194304 | tf_op jit(solution)/shard_map/reshape | solution.py:164
  269.4 3.2 pad_maximum_fusion
  272.5 4.4 all-to-all-start.1
  276.9 4.1 fusion.6
  281.1 25.3 %all-to-all-done.1 = bf16[8,256,576]{1,2,0:T(8,128)(2,1)} async-done(((bf16[8,256,576]{1,2,0:T(8,128)(2,1)}), bf16[8,256,576]{1,2,0:T(8,128)(2,1)}, u32[]{:S(2)}, u32[]{:S(2)}) %all-to-all-start.1) | async-done | bytes 2359328 | tf_op jit(solution)/shard_map/all_to_all | solution.py:173
  306.3 4.5 stack.5
  310.9 5.3 %all-to-all-start.2 = ((bf16[4,768,1024]{1,2,0:T(8,128)(2,1)}), bf16[4,768,1024]{1,2,0:T(8,128)(2,1)}, u32[]{:S(2)}, u32[]{:S(2)}) async-start(bf16[4,768,1024]{1,2,0:T(8,128)(2,1)} %stack.5), calls=%async_computation.2 | async-start | bytes 12582912 | tf_op jit(solution)/shard_map/all_to_all | solution.py:149
  316.1 0.0 all-reduce.5.cloned.1.call-start
  316.2 0.3 fusion.17
  316.5 72.0 %all_gather.29 = bf16[1024,64]{0,1:T(8,128)(2,1)S(1)} all-gather(bf16[256,64]{0,1:T(8,128)(2,1)S(1)} %fusion.17), channel_id=1, replica_groups=mesh['grp'=4,'fsdp'=4,'tp'=2] {'fsdp'}, dimensions={0}, use_global_device_ids=true | all-gather | bytes 163840 | tf_op jit(solution)/shard_map/all_gather | solution.py:111
  388.5 1.2 fusion.44
  389.7 2.1 reduce.1
  391.8 0.2 convolution_multiply_fusion.1
  392.0 0.1 reshape.78
  392.1 0.8 copy.63
  392.9 0.0 all-gather.10.cloned.1.call-start
  392.9 37.2 %all-reduce.5.cloned.1.call-done = (f32[512,64]{0,1:T(8,128)}, f32[1024,64]{0,1:T(8,128)}) async-done(((f32[512,64]{0,1:T(8,128)}, f32[1024,64]{0,1:T(8,128)}), (f32[512,64]{0,1:T(8,128)}, f32[1024,64]{0,1:T(8,128)})) %all-reduce.5.cloned.1.call-update) | async-done | bytes 393232 | tf_op jit(solution)/shard_map/psum | solution.py:179
  430.1 1.8 pad_maximum_fusion.1
  431.9 0.8 copy.65
  432.8 14.6 %convolution_bitcast_fusion = f32[1280,4096]{0,1:T(8,128)} fusion(bf16[768,4096]{0,1:T(8,128)(2,1)} %bitcast.12, bf16[768,1280]{1,0:T(8,128)(2,1)S(1)} %copy-done.3), kind=kOutput, calls=%fused_computation | convolution fusion | flops 8053063680 | bytes 29229056 | tf_op jit(solution)/shard_map/dot_general | solution.py:12
  447.4 22.4 %copy.66 = f32[1280,4096]{1,0:T(8,128)} copy(f32[1280,4096]{0,1:T(8,128)} %convolution_bitcast_fusion) | data formatting | bytes 41943040
  469.8 2.4 reshape.83
  472.2 0.2 slice_reduce_fusion
  472.4 0.1 slice.55
  472.6 1.6 copy.71
  474.2 0.1 copy.64
  474.3 0.8 reshape.80
  (38 shorter events, 0.4 us)
Async XLA Ops:
  7.2 149.1 %copy-start = (bf16[2048,64]{0,1:T(8,128)(2,1)S(1)}, bf16[2048,64]{0,1:T(8,128)(2,1)}, u32[]{:S(2)}) copy-start(bf16[2048,64]{0,1:T(8,128)(2,1)} %param.17) | copy-start | bytes 786436
  7.2 39.5 %all-gather.6.cloned.1.call-start = ((), (), s32[]{:S(2)}) async-start(), calls=%async_computation.3 | async-start | bytes 2457600 | tf_op jit(solution)/shard_map/all_gather | solution.py:57
  7.9 126.6 %all-reduce.7.cloned.1.call-start = ((), (), s32[]{:S(2)}) async-start(), calls=%async_computation.7 | async-start | bytes 3932160 | tf_op jit(solution)/shard_map/psum | solution.py:117
  52.5 158.7 %all-gather.8.cloned.1.call-start = ((), (), s32[]{:S(2)}) async-start(), calls=%async_computation.4 | async-start | bytes 1966080 | tf_op jit(solution)/shard_map/all_gather | solution.py:113
  140.2 66.4 %all-to-all-start = ((bf16[4,256,1024]{2,1,0:T(8,128)(2,1)}), bf16[4,256,1024]{2,1,0:T(8,128)(2,1)S(1)}, u32[]{:S(2)}, u32[]{:S(2)}) async-start(bf16[4,256,1024]{2,1,0:T(8,128)(2,1)} %bitcast.63), calls=%async_computation | async-start | bytes 4194304 | tf_op jit(solution)/shard_map/all_to_all | solution.py:59
  146.8 10.9 %collective-permute-start = (bf16[1024,512]{1,0:T(8,128)(2,1)}, bf16[1024,512]{1,0:T(8,128)(2,1)}, u32[]{:S(2)}, u32[]{:S(2)}) collective-permute-start(bf16[1024,512]{1,0:T(8,128)(2,1)} %get-tuple-element.30), channel_id=1, source_target_pairs={{0,0},{1,2},{2,4},{3,6},{4,1},{5,3},{6,5},{7,7},{8,8},{9,10},{10,1... | collective-permute-start | bytes 3145736 | tf_op jit(solution)/shard_map/ppermute | solution.py:71
  156.3 45.4 %collective-permute-start.1 = (bf16[1024,512]{1,0:T(8,128)(2,1)}, bf16[1024,512]{1,0:T(8,128)(2,1)}, u32[]{:S(2)}, u32[]{:S(2)}) collective-permute-start(bf16[1024,512]{1,0:T(8,128)(2,1)} %get-tuple-element.29), channel_id=1, source_target_pairs={{0,2},{1,0},{2,6},{3,4},{4,3},{5,1},{6,7},{7,5},{8,10},{9,8},{10,1... | collective-permute-start | bytes 3145736 | tf_op jit(solution)/shard_map/ppermute | solution.py:71
  156.3 54.8 %collective-permute-start.2 = (bf16[1024,64]{0,1:T(8,128)(2,1)S(1)}, bf16[1024,64]{0,1:T(8,128)(2,1)S(1)}, u32[]{:S(2)}, u32[]{:S(2)}) collective-permute-start(bf16[1024,64]{0,1:T(8,128)(2,1)S(1)} %constant_dynamic-slice_fusion.2), channel_id=1, source_target_pairs={{0,0},{1,2},{2,4},{3,6},{4,1},{5,3},{6,5},{7,7},{8,8},{9,10},{10,1... | collective-permute-start | bytes 393224 | tf_op jit(solution)/shard_map/ppermute | solution.py:78
  211.1 4.3 copy-start.2
  272.5 33.8 %all-to-all-start.1 = ((bf16[8,256,576]{1,2,0:T(8,128)(2,1)}), bf16[8,256,576]{1,2,0:T(8,128)(2,1)}, u32[]{:S(2)}, u32[]{:S(2)}) async-start(bf16[8,256,576]{1,2,0:T(8,128)(2,1)} %bitcast.62), calls=%async_computation.1 | async-start | bytes 4718592 | tf_op jit(solution)/shard_map/all_to_all | solution.py:173
  310.9 121.9 %all-to-all-start.2 = ((bf16[4,768,1024]{1,2,0:T(8,128)(2,1)}), bf16[4,768,1024]{1,2,0:T(8,128)(2,1)}, u32[]{:S(2)}, u32[]{:S(2)}) async-start(bf16[4,768,1024]{1,2,0:T(8,128)(2,1)} %stack.5), calls=%async_computation.2 | async-start | bytes 12582912 | tf_op jit(solution)/shard_map/all_to_all | solution.py:149
  316.1 113.9 %all-reduce.5.cloned.1.call-start = ((), (), s32[]{:S(2)}) async-start(), calls=%async_computation.6 | async-start | bytes 786432 | tf_op jit(solution)/shard_map/psum | solution.py:179
  391.8 41.0 %copy-start.3 = (bf16[768,1280]{1,0:T(8,128)(2,1)S(1)}, bf16[768,1280]{1,0:T(8,128)(2,1)}, u32[]{:S(2)}) copy-start(bf16[768,1280]{1,0:T(8,128)(2,1)} %all-gather.6.cloned.1.call-done) | copy-start | bytes 5898244
  392.9 76.9 %all-gather.10.cloned.1.call-start = ((), (), s32[]{:S(2)}) async-start(), calls=%async_computation.5 | async-start | bytes 1966080 | tf_op jit(solution)/shard_map/all_gather | solution.py:180
  472.2 2.9 copy-start.1
Sparse Core Ops, SparseCore 0:
  9.8 36.8 all-gather.5
  52.6 81.8 all-reduce.6
  136.3 52.9 all-gather.7
  393.0 37.0 all-reduce.4
  432.3 30.4 all-gather.9
